TPU v7x, 32 devices: a whole 2x2x4 slice. The times are simulated.
32 devices in a mesh: rows: 4 (over y, x), mp: 8 (over z, core).
Axes of the slice: x: 2, y: 2, z: 4, core: 2. Of those that a mesh axis runs over, the one named last changes fastest.
Arguments:
- tokens: bfloat16 [512, 6144], P('rows', 'mp'), may hold values from -8 to 8
- norm_gain: float32 [6144], replicated, may hold values from 0.25 to 1.75
- hidden_bias: float32 [24576], P('mp'), may hold values from -3 to 3
- weight_in: bfloat16 [6144, 24576], P('rows', 'mp'), may hold values from -0.078125 to 0.078125
- weight_out: bfloat16 [24576, 6144], P('mp', 'rows'), may hold values from -0.0546875 to 0.0546875
Outputs:
- updated: bfloat16 [512, 6144], P('rows', 'mp')
All inputs are finite; a program needn't handle non-finite values.
Results may differ from a plain program's by a relative error of at most 0.0041.
Values may be sent and summed in bfloat16 or wider, within the bound.
A program may use at most 128 MiB of HBM per device.

v0:
```python
import functools

import jax
import jax.numpy as jnp
from jax import lax
from jax.experimental import pallas as pl
from jax.experimental.pallas import tpu as pltpu
from jax.sharding import PartitionSpec as P

MESH = pl.DeviceIdType.MESH
F32 = jnp.float32
BF16 = jnp.bfloat16
floor_value = 0.1
CHUNKS = 4


def gelu(x):
    return 0.5 * x * (1.0 + lax.erf(x * 0.7071067811865476))


def kernel(
    R, M, K, D, tok, gain, bias, win_hbm, wout_hbm, out, win, wout, xs, nx, stat, pbuf, r1, r2, qbuf, hid,
    osend, osib, oown, zlo, zhi, zsend, fsend, fbuf, wsem,
    s_src, s_dn, s_up, s_sib, r_x, r_xs, s_st, r_st, s_r1, r_r1, s_r2, r_r2, s_ag, r_ag, s_os, r_os, s_z, r_zl, r_zh,
    s_f, r_f,
):
    r = lax.axis_index("rows")
    m = lax.axis_index("mp")
    Z = M // 2
    z, c = m // 2, m % 2
    sib = 2 * z + 1 - c
    rows = tok.shape[0] // K
    width = tok.shape[1]
    half = win.shape[1] // 2
    rx, ry, rd = r + 1 - 2 * (r % 2), (r + 2) % 4, 3 - r
    first, second = (rx, ry), (ry, rx)
    peers = (rx, ry, rd)

    pltpu.make_async_copy(win_hbm, win, wsem.at[0]).start()
    pltpu.make_async_copy(wout_hbm, wout, wsem.at[1]).start()

    barrier = pltpu.get_barrier_semaphore()
    for peer in peers:
        pl.semaphore_signal(barrier, inc=1, device_id=(peer, m), device_id_type=MESH)
    pl.semaphore_signal(barrier, inc=1, device_id=(r, sib), device_id_type=MESH)

    @pl.when(z > 0)
    def _():
        pl.semaphore_signal(barrier, inc=1, device_id=(r, m - 2), device_id_type=MESH)

    @pl.when(z < Z - 1)
    def _():
        pl.semaphore_signal(barrier, inc=1, device_id=(r, m + 2), device_id_type=MESH)

    pl.semaphore_wait(barrier, 4 + jnp.where(z > 0, 1, 0) + jnp.where(z < Z - 1, 1, 0))

    def remote(src, dst, ssem, rsem, row, col):
        return pltpu.make_async_remote_copy(
            src_ref=src, dst_ref=dst, send_sem=ssem, recv_sem=rsem, device_id=(row, col), device_id_type=MESH
        )

    def c_src(k):
        return remote(tok.at[pl.ds(k * rows, rows)], xs.at[k, r, c], s_src.at[k], r_x.at[k, r], z, m)

    def c_x(k, t, col, ssem):
        return remote(xs.at[k, t, c], xs.at[k, t, c], ssem.at[k, t], r_x.at[k, t], r, col)

    def c_sib(k, t):
        return remote(xs.at[k, t, c], xs.at[k, t, c], s_sib.at[k, t], r_xs.at[k, t], r, sib)

    def w_sib(k, t):
        return remote(xs.at[k, t, 1 - c], xs.at[k, t, 1 - c], s_sib.at[k, t], r_xs.at[k, t], r, sib)

    def c_st(k, i):
        return remote(stat.at[k, r], stat.at[k, r], s_st.at[k, i], r_st.at[k, r], peers[i], m)

    def w_st(k, i):
        return remote(stat.at[k, peers[i]], stat.at[k, peers[i]], s_st.at[k, i], r_st.at[k, peers[i]], peers[i], m)

    def c_r1(k, h, i):
        tile = (first[h], rd)[i]
        return remote(pbuf.at[k, h, tile], r1.at[k, h, i], s_r1.at[k, h, i], r_r1.at[k, h, i], first[h], m)

    def c_r2(k, h):
        return remote(qbuf.at[k, h], r2.at[k, h], s_r2.at[k, h], r_r2.at[k, h], second[h], m)

    def c_ag(k, h, i):
        tile = (r, r, second[h])[i]
        to = (second[h], first[h], first[h])[i]
        return remote(hid.at[k, h, tile], hid.at[k, h, tile], s_ag.at[k, h, i], r_ag.at[k, h, tile], to, m)

    def w_ag(k, h, tile):
        return remote(hid.at[k, h, tile], hid.at[k, h, tile], s_ag.at[k, h, 0], r_ag.at[k, h, tile], first[h], m)

    def c_os(k):
        return remote(osend.at[k], osib.at[k], s_os.at[k], r_os.at[k], r, sib)

    def c_zl(k, t, col):
        return remote(zsend.at[k, t], zlo.at[k, t], s_z.at[k, t], r_zl.at[k, t], r, col)

    def c_zh(k, t, col):
        return remote(zsend.at[k, t], zhi.at[k, t], s_z.at[k, t], r_zh.at[k, t], r, col)

    def c_f(k, t):
        return remote(fsend.at[k, t], fbuf.at[k], s_f.at[k, t], r_f.at[k], t, m)

    home = z == r
    has_dn = (z <= r) & (z > 0)
    has_up = (z >= r) & (z < Z - 1)

    @pl.when(home)
    def _():
        for k in range(K):
            xs[k, r, c] = tok[k * rows:(k + 1) * rows]

    @pl.when(jnp.logical_not(home))
    def _():
        for k in range(K):
            c_src(k).start()

    def stage_a(k):
        for t in range(R):
            @pl.when(jnp.logical_not(home & (r == t)))
            def _():
                c_x(k, t, sib, s_dn).wait_recv()

            @pl.when(has_dn)
            def _():
                c_x(k, t, m - 2, s_dn).start()

            @pl.when(has_up)
            def _():
                c_x(k, t, m + 2, s_up).start()

            c_sib(k, t).start()

    def chunk_x(k, cc):
        return xs[k, :, cc].astype(F32).reshape(R * rows, width)

    def stage_s(k):
        for t in range(R):
            w_sib(k, t).wait_recv()
        s1 = 0.0
        s2 = 0.0
        for cc in range(2):
            x = chunk_x(k, cc)
            s1 = s1 + jnp.sum(x, axis=1, keepdims=True)
            s2 = s2 + jnp.sum(x * x, axis=1, keepdims=True)
        lane = lax.broadcasted_iota(jnp.int32, (R * rows, 128), 1)
        both = jnp.where(lane == 0, s1, s2)
        stat[k, r] = both.T[0:8]
        for i in range(3):
            c_st(k, i).start()

    def stage_m1(k):
        for i in range(3):
            w_st(k, i).wait_recv()
        tot = (stat[k, 0] + stat[k, 1]) + (stat[k, 2] + stat[k, 3])
        mean = tot[0:1] / D
        var = jnp.maximum(tot[1:2] / D - mean * mean, 0.0)
        inv = lax.rsqrt(var + floor_value)
        sub = lax.broadcasted_iota(jnp.int32, (128, R * rows), 0)
        cols = jnp.where(sub == 0, mean, inv).T
        mean_c, inv_c = cols[:, 0:1], cols[:, 1:2]
        for cc in range(2):
            nx[cc] = ((chunk_x(k, cc) - mean_c) * inv_c * gain[2 * r + cc]).astype(BF16)

        @pl.when(k == 0)
        def _():
            pltpu.make_async_copy(win_hbm, win, wsem.at[0]).wait()

        tile = half // 2

        for h in range(2):
            def col(j, _):
                at = pl.multiple_of(j * tile, 128)
                wat = pl.multiple_of(h * half + j * tile, 128)
                acc = jnp.dot(nx[0], win[0:width, pl.ds(wat, tile)], preferred_element_type=F32)
                acc += jnp.dot(nx[1], win[width:2 * width, pl.ds(wat, tile)], preferred_element_type=F32)
                pbuf[k, h, :, :, pl.ds(at, tile)] = acc.astype(BF16).reshape(R, rows, tile)
                return 0

            lax.fori_loop(0, 2, col, 0)
            c_r1(k, h, 1).start()
            c_r1(k, h, 0).start()

    def stage_b1(k):
        for h in range(2):
            c_r1(k, h, 1).wait_recv()
            qbuf[k, h] = (pbuf[k, h, second[h]].astype(F32) + r1[k, h, 1].astype(F32)).astype(BF16)
            c_r2(k, h).start()

    def stage_b2(k):
        for h in range(2):
            c_r1(k, h, 0).wait_recv()
            c_r2(k, h).wait_recv()
            pre = pbuf[k, h, r].astype(F32) + r1[k, h, 0].astype(F32) + r2[k, h].astype(F32)
            pre = pre + bias[0:1, h * half:(h + 1) * half]
            hid[k, h, r] = gelu(pre).astype(BF16)
            c_ag(k, h, 0).start()
            c_ag(k, h, 1).start()

    def stage_b3(k):
        for h in range(2):
            w_ag(k, h, second[h]).wait_recv()
            c_ag(k, h, 2).start()

    def stage_b4(k):
        for h in range(2):
            w_ag(k, h, first[h]).wait_recv()
            w_ag(k, h, rd).wait_recv()

        @pl.when(k == 0)
        def _():
            pltpu.make_async_copy(wout_hbm, wout, wsem.at[1]).wait()

        def product(cc):
            at = pl.multiple_of(cc * width, 128)
            acc = None
            for h in range(2):
                a = hid[k, h].reshape(R * rows, half)
                part = jnp.dot(a, wout[h * half:(h + 1) * half, pl.ds(at, width)], preferred_element_type=F32)
                acc = part if acc is None else acc + part
            return acc.reshape(R, rows, width)

        osend[k] = product(1 - c).astype(BF16)
        c_os(k).start()
        oown[k] = product(c)

    def stage_c(k):
        c_os(k).wait_recv()
        for t in range(R):
            oown[k, t] = oown[k, t] + osib[k, t].astype(F32)

            @pl.when(has_dn)
            def _():
                c_zl(k, t, sib).wait_recv()
                oown[k, t] = oown[k, t] + zlo[k, t].astype(F32)

            @pl.when(has_up)
            def _():
                c_zh(k, t, sib).wait_recv()
                oown[k, t] = oown[k, t] + zhi[k, t].astype(F32)

            @pl.when(home)
            def _():
                done = (xs[k, t, c].astype(F32) + oown[k, t]).astype(BF16)

                @pl.when(r == t)
                def _():
                    fbuf[k] = done

                @pl.when(r != t)
                def _():
                    fsend[k, t] = done
                    c_f(k, t).start()

            @pl.when(jnp.logical_not(home))
            def _():
                zsend[k, t] = oown[k, t].astype(BF16)

            @pl.when(z < r)
            def _():
                c_zl(k, t, m + 2).start()

            @pl.when(z > r)
            def _():
                c_zh(k, t, m - 2).start()

    def at_chunk(k, fn):
        @pl.when((k >= 0) & (k < K))
        def _():
            fn(k)

    behind = jnp.where(z < r, z, jnp.where(z > r, Z - 1 - z, jnp.maximum(z, Z - 1 - z)))
    lead = jnp.minimum(Z - 1 - jnp.maximum(z - r, r - z), K - 1)

    def ahead(k, _):
        stage_a(k)
        return 0

    lax.fori_loop(0, lead + 1, ahead, 0)
    stage_s(0)

    def step(t, _):
        at_chunk(t + 1 + lead, stage_a)
        at_chunk(t + 1, stage_s)
        at_chunk(t - 1, stage_b1)
        at_chunk(t, stage_m1)
        at_chunk(t - 2, stage_b3)
        at_chunk(t - 1, stage_b2)
        at_chunk(t - 2, stage_b4)
        at_chunk(t - 2 - behind, stage_c)
        return 0

    lax.fori_loop(0, K + 2 + Z - 1, step, 0)

    def drain(k, _):
        for t in range(R):
            @pl.when(has_dn)
            def _():
                c_x(k, t, sib, s_dn).wait_send()

            @pl.when(has_up)
            def _():
                c_x(k, t, sib, s_up).wait_send()

            c_sib(k, t).wait_send()

            @pl.when(home & (r != t))
            def _():
                c_f(k, t).wait_send()

            @pl.when(jnp.logical_not(home))
            def _():
                c_zl(k, t, sib).wait_send()

        @pl.when(jnp.logical_not(home))
        def _():
            c_src(k).wait_send()
            c_f(k, rx).wait_recv()

        for i in range(3):
            c_st(k, i).wait_send()
        for h in range(2):
            c_r1(k, h, 0).wait_send()
            c_r1(k, h, 1).wait_send()
            c_r2(k, h).wait_send()
            for i in range(3):
                c_ag(k, h, i).wait_send()
        c_os(k).wait_send()
        return 0

    lax.fori_loop(0, K, drain, 0)
    for k in range(K):
        out[k * rows:(k + 1) * rows] = fbuf[k]


def fused(tokens, norm_gain, hidden_bias, weight_in, weight_out, R, M, D, K):
    height, width = tokens.shape
    depth, ff = weight_in.shape
    rows, half = height // K, ff // 2
    V = pltpu.VMEM
    S = pltpu.SemaphoreType.DMA
    vm = pl.BlockSpec(memory_space=pltpu.VMEM)
    hbm = pl.BlockSpec(memory_space=pltpu.HBM)
    return pl.pallas_call(
        functools.partial(kernel, R, M, K, D),
        out_shape=jax.ShapeDtypeStruct(tokens.shape, BF16),
        in_specs=[vm, vm, vm, hbm, hbm],
        out_specs=vm,
        scratch_shapes=[
            V(weight_in.shape, BF16), V(weight_out.shape, BF16),
            V((K, R, 2, rows, width), BF16), V((2, R * rows, width), BF16), V((K, R, 8, R * rows), F32),
            V((K, 2, R, rows, half), BF16), V((K, 2, 2, rows, half), BF16), V((K, 2, rows, half), BF16),
            V((K, 2, rows, half), BF16), V((K, 2, R, rows, half), BF16),
            V((K, R, rows, width), BF16), V((K, R, rows, width), BF16), V((K, R, rows, width), F32),
            V((K, R, rows, width), BF16), V((K, R, rows, width), BF16), V((K, R, rows, width), BF16),
            V((K, R, rows, width), BF16), V((K, rows, width), BF16), S((2,)),
            S((K,)), S((K, R)), S((K, R)), S((K, R)), S((K, R)), S((K, R)), S((K, 3)), S((K, R)),
            S((K, 2, 2)), S((K, 2, 2)), S((K, 2)), S((K, 2)), S((K, 2, 3)), S((K, 2, R)), S((K,)), S((K,)),
            S((K, R)), S((K, R)), S((K, R)), S((K, R)), S((K,)),
        ],
        compiler_params=pltpu.CompilerParams(
            collective_id=0, has_side_effects=True, vmem_limit_bytes=60 * 1024 * 1024
        ),
    )(tokens, norm_gain.reshape(M, 1, width), hidden_bias.reshape(1, ff), weight_in, weight_out)


def plain(tokens, norm_gain, hidden_bias, weight_in, weight_out, R, M, D):
    as_float = tokens.astype(F32)
    moment_sum, square_sum = lax.psum((jnp.sum(as_float, axis=1), jnp.sum(as_float * as_float, axis=1)), "mp")
    width = tokens.shape[1]
    gain = lax.dynamic_slice_in_dim(norm_gain, lax.axis_index("mp") * width, width)
    mean = moment_sum / D
    inverse = lax.rsqrt(jnp.maximum(square_sum / D - mean * mean, 0.0) + floor_value)
    part = ((as_float - mean[:, None]) * inverse[:, None] * gain[None, :]).astype(BF16)
    normed = lax.all_gather(part, "mp", axis=1, tiled=True)
    shuffled = lax.all_to_all(normed, "rows", split_axis=1, concat_axis=0, tiled=True)
    preact = lax.psum_scatter(
        jnp.dot(shuffled, weight_in, preferred_element_type=F32), "rows", scatter_dimension=0, tiled=True
    )
    hidden = jax.nn.gelu(preact + hidden_bias[None, :], approximate=False).astype(BF16)
    hidden = lax.all_gather(hidden, "rows", axis=0, tiled=True)
    terms = jnp.dot(hidden, weight_out, preferred_element_type=F32)
    terms = lax.all_to_all(terms, "rows", split_axis=0, concat_axis=1, tiled=True)
    branch = lax.psum_scatter(terms, "mp", scatter_dimension=1, tiled=True)
    return (as_float + branch).astype(BF16)


def solution(mesh):
    R, M = mesh.shape["rows"], mesh.shape["mp"]

    def body(tokens, norm_gain, hidden_bias, weight_in, weight_out):
        D = norm_gain.shape[0]
        aligned = tokens.shape[1] % 128 == 0 and weight_in.shape[1] % 512 == 0 and tokens.shape[0] % (32 * CHUNKS) == 0
        if R == 4 and M == 2 * R and aligned:
            return fused(tokens, norm_gain, hidden_bias, weight_in, weight_out, R, M, D, CHUNKS)
        return plain(tokens, norm_gain, hidden_bias, weight_in, weight_out, R, M, D)

    return jax.shard_map(
        body,
        mesh=mesh,
        in_specs=(P("rows", "mp"), P(), P("mp"), P("rows", "mp"), P("mp", "rows")),
        out_specs=P("rows", "mp"),
        check_vma=False,
    )
```

profile of v0, /device:TPU:0, one launch (start us, length us, event | category | flops | bytes accessed | tf_op | source)
XLA Modules:
  0.0 111.2 jit_solution(9069358787551186642)
XLA Ops:
  0.0 109.5 %shard_map.55 = bf16[128,768]{1,0:T(8,128)(2,1)} custom-call(bf16[128,768]{1,0:T(8,128)(2,1)} %tok.1, f32[8,1,768]{2,1,0:T(1,128)} %bitcast.2, f32[1,3072]{1,0:T(1,128)} %bitcast.3, bf16[1536,3072]{1,0:T(8,128)(2,1)} %win_hbm.1, bf16[3072,1536]{1,0:T(8,128)(2,1)} %wout_hbm.1), custom_call_target="tpu_custom_call" | custom-call | tf_op jit(solution)/shard_map/pallas_call | solution.py:347
  109.6 1.6 %copy.7 = bf16[128,768]{1,0:T(8,128)(2,1)} copy(bf16[128,768]{1,0:T(8,128)(2,1)} %shard_map.55) | data formatting | bytes 393216
where the time goes:
time: 111 us
  Pallas kernels  110 us (99%)
  local copies, waits for them, and re-layouts  1.62 us (1%)
    pallas_call x1, Pallas kernels, fused(): pl.pallas_call(functools.partial(kernel, R, M, K, D), out_shape=jax.Shape...  110 us

commit v1 on v0

v1 whole, which is shorter than its diff:
```python
import functools

import jax
import jax.numpy as jnp
from jax import lax
from jax.experimental import pallas as pl
from jax.experimental.pallas import tpu as pltpu
from jax.sharding import PartitionSpec as P

MESH = pl.DeviceIdType.MESH
F32 = jnp.float32
BF16 = jnp.bfloat16
floor_value = 0.1
UNITS = (1, 2, 2, 2, 1)


def gelu(x):
    return 0.5 * x * (1.0 + lax.erf(x * 0.7071067811865476))


def kernel(
    R, M, D, cuts, order, tok, gain, bias, win_hbm, wout_hbm, out, win, wout, xs, nx, stc, mi, colst,
    pbuf, r1, r2, qbuf, hid, osend, osib, oown, csend, cmid, crecv, wsem,
    s_a, r_a, s_sib, r_sib, s_st, r_st, s_mi, r_mi, s_r1, r_r1, s_r2, r_r2, s_ag, r_ag, s_os, r_os,
    s_cm, r_cm, s_cz, r_cz,
):
    r = lax.axis_index("rows")
    m = lax.axis_index("mp")
    Z = M // 2
    z, c = m // 2, m % 2
    sib = 2 * z + 1 - c
    height, width = tok.shape
    half = win.shape[1] // 2
    K = len(cuts)
    offs = [sum(cuts[:k]) for k in range(K)]
    rx, ry, rd = r + 1 - 2 * (r % 2), (r + 2) % 4, 3 - r
    first, second = (rx, ry), (ry, rx)
    peers = (rd, rx, ry)
    home = z == r

    pltpu.make_async_copy(win_hbm, win, wsem.at[0]).start()
    pltpu.make_async_copy(wout_hbm, wout, wsem.at[1]).start()

    def remote(src, dst, ssem, rsem, row, col):
        return pltpu.make_async_remote_copy(
            src_ref=src, dst_ref=dst, send_sem=ssem, recv_sem=rsem, device_id=(row, col), device_id_type=MESH
        )

    def part(k):
        return pl.ds(offs[k], cuts[k])

    barrier = pltpu.get_barrier_semaphore()

    def greet(row, col):
        pl.semaphore_signal(barrier, inc=1, device_id=(row, col), device_id_type=MESH)

    for i in range(1, M):
        greet(r, (m + i) % M)
    for i in range(1, R):
        greet((r + i) % R, m)

    @pl.when(jnp.logical_not(home))
    def _():
        for i in range(1, R):
            greet((r + i) % R, 2 * r + c)

    own = tok[...].astype(F32)
    lane = lax.broadcasted_iota(jnp.int32, (height, 128), 1)
    s1 = jnp.sum(own, axis=1, keepdims=True)
    s2 = jnp.sum(own * own, axis=1, keepdims=True)
    stc[m] = jnp.where(lane == 0, s1, s2).T[0:8]

    pl.semaphore_wait(barrier, (M - 1) + (R - 1) + jnp.where(home, 0, R - 1))

    toward = 2 * (z // 2) - 1

    def c_a(k, i):
        zd = (z + i * toward + Z) % Z
        return remote(tok.at[part(k)], xs.at[c, r, part(k)], s_a.at[k, i], r_a.at[k, r], z, 2 * zd + c)

    def c_sib(k, t, src):
        return remote(src, xs.at[c, t, part(k)], s_sib.at[k, t], r_sib.at[k, t], r, sib)

    def c_st(i):
        return remote(stc.at[m], stc.at[m], s_st.at[i], r_st.at[m], r, (m + i) % M)

    def c_mi(i):
        return remote(mi.at[r], mi.at[r], s_mi.at[i], r_mi.at[r], peers[i], m)

    def c_r1(k, h, i):
        tile = (first[h], rd)[i]
        return remote(
            pbuf.at[h, tile, part(k)], r1.at[h, i, part(k)], s_r1.at[k, h, i], r_r1.at[k, h, i], first[h], m
        )

    def c_r2(k, h):
        return remote(qbuf.at[h, part(k)], r2.at[h, part(k)], s_r2.at[k, h], r_r2.at[k, h], second[h], m)

    def c_ag(k, h, i):
        tile = (r, r, second[h])[i]
        to = (second[h], first[h], first[h])[i]
        ref = hid.at[h, tile, part(k)]
        return remote(ref, ref, s_ag.at[k, h, i], r_ag.at[k, h, tile], to, m)

    def w_ag(k, h, tile):
        ref = hid.at[h, tile, part(k)]
        return remote(ref, ref, s_ag.at[k, h, 0], r_ag.at[k, h, tile], first[h], m)

    def c_os(k):
        return remote(osend.at[:, part(k)], osib.at[:, part(k)], s_os.at[k], r_os.at[k], r, sib)

    def c_cm(k, i):
        t = peers[i]
        return remote(csend.at[t, part(k)], cmid.at[r, part(k)], s_cm.at[k, i], r_cm.at[k, r], t, m)

    def c_cz(k, q, src):
        return remote(src, crecv.at[z, part(k)], s_cz.at[k, q], r_cz.at[k, z], r, 2 * q + c)

    def stage_send(k):
        for i in range(1, Z):
            c_a(k, i).start()

        @pl.when(home)
        def _():
            xs[c, r, part(k)] = tok[part(k)]
            c_sib(k, r, tok.at[part(k)]).start()

        @pl.when(jnp.logical_not(home))
        def _():
            c_a(k, 0).start()

    def stage_st0(_):
        for i in range(1, M):
            c_st(i).start()

    def stage_st1(_):
        for i in range(1, M):
            q = (m + i) % M
            remote(stc.at[q], stc.at[q], s_st.at[i], r_st.at[q], r, q).wait_recv()
        tot = stc[0]
        for q in range(1, M):
            tot = tot + stc[q]
        mean = tot[0:1] / D
        var = jnp.maximum(tot[1:2] / D - mean * mean, 0.0)
        inv = lax.rsqrt(var + floor_value)
        sub = lax.broadcasted_iota(jnp.int32, (8, height), 0)
        mi[r] = jnp.where(sub == 0, mean, inv)
        for i in range(3):
            c_mi(i).start()

    def stage_st2(_):
        for i in range(3):
            p = peers[i]
            remote(mi.at[p], mi.at[p], s_mi.at[i], r_mi.at[p], p, m).wait_recv()
        sub = lax.broadcasted_iota(jnp.int32, (128, height), 0)
        for t in range(R):
            colst[t] = jnp.where(sub == 0, mi[t, 0:1], mi[t, 1:2]).T

    def stage_a(k):
        for i in range(R):
            t = (r + i) % R
            if i == 0:
                @pl.when(jnp.logical_not(home))
                def _():
                    remote(tok.at[part(k)], xs.at[c, r, part(k)], s_a.at[k, 0], r_a.at[k, r], r, sib).wait_recv()
                    c_sib(k, r, xs.at[c, r, part(k)]).start()
            else:
                remote(tok.at[part(k)], xs.at[c, t, part(k)], s_a.at[k, 0], r_a.at[k, t], r, sib).wait_recv()
                c_sib(k, t, xs.at[c, t, part(k)]).start()

    def stage_m1(k):
        n = cuts[k]
        for t in range(R):
            ref = xs.at[1 - c, t, part(k)]
            remote(ref, ref, s_sib.at[k, t], r_sib.at[k, t], r, sib).wait_recv()
        stats = colst[:, part(k)].reshape(R * n, 128)
        mean_c, inv_c = stats[:, 0:1], stats[:, 1:2]
        for cc in range(2):
            x = xs[cc, :, part(k)].astype(F32).reshape(R * n, width)
            nx[cc, 0:R * n] = ((x - mean_c) * inv_c * gain[2 * r + cc]).astype(BF16)

        if k == 0:
            pltpu.make_async_copy(win_hbm, win, wsem.at[0]).wait()

        tile = half // 2
        for h in range(2):
            def col(j, _):
                at = pl.multiple_of(j * tile, 128)
                wat = pl.multiple_of(h * half + j * tile, 128)
                acc = jnp.dot(nx[0, 0:R * n], win[0:width, pl.ds(wat, tile)], preferred_element_type=F32)
                acc += jnp.dot(nx[1, 0:R * n], win[width:2 * width, pl.ds(wat, tile)], preferred_element_type=F32)
                pbuf[h, :, part(k), pl.ds(at, tile)] = acc.astype(BF16).reshape(R, n, tile)
                return 0

            lax.fori_loop(0, 2, col, 0)
            c_r1(k, h, 1).start()
            c_r1(k, h, 0).start()

    def stage_b1(k):
        for h in range(2):
            c_r1(k, h, 1).wait_recv()
            mine = pbuf[h, second[h], part(k)].astype(F32)
            qbuf[h, part(k)] = (mine + r1[h, 1, part(k)].astype(F32)).astype(BF16)
            c_r2(k, h).start()

    def stage_b2(k):
        for h in range(2):
            c_r1(k, h, 0).wait_recv()
            c_r2(k, h).wait_recv()
            pre = pbuf[h, r, part(k)].astype(F32) + r1[h, 0, part(k)].astype(F32) + r2[h, part(k)].astype(F32)
            pre = pre + bias[0:1, h * half:(h + 1) * half]
            hid[h, r, part(k)] = gelu(pre).astype(BF16)
            c_ag(k, h, 0).start()
            c_ag(k, h, 1).start()

    def stage_b3(k):
        for h in range(2):
            w_ag(k, h, second[h]).wait_recv()
            c_ag(k, h, 2).start()

    def stage_b4(k):
        n = cuts[k]
        for h in range(2):
            w_ag(k, h, first[h]).wait_recv()
            w_ag(k, h, rd).wait_recv()

        if k == 0:
            pltpu.make_async_copy(wout_hbm, wout, wsem.at[1]).wait()

        def product(cc):
            at = pl.multiple_of(cc * width, 128)
            acc = None
            for h in range(2):
                a = hid[h, :, part(k)].reshape(R * n, half)
                term = jnp.dot(a, wout[h * half:(h + 1) * half, pl.ds(at, width)], preferred_element_type=F32)
                acc = term if acc is None else acc + term
            return acc.reshape(R, n, width)

        osend[:, part(k)] = product(1 - c).astype(BF16)
        c_os(k).start()
        oown[:, part(k)] = product(c)

    def stage_c1(k):
        c_os(k).wait_recv()
        csend[:, part(k)] = (oown[:, part(k)] + osib[:, part(k)].astype(F32)).astype(BF16)
        for i in range(3):
            c_cm(k, i).start()

        @pl.when(jnp.logical_not(home))
        def _():
            c_cz(k, r, csend.at[r, part(k)]).start()

    def stage_c2(k):
        for i in (1, 2, 0):
            q = peers[i]
            remote(csend.at[r, part(k)], cmid.at[q, part(k)], s_cm.at[k, i], r_cm.at[k, q], q, m).wait_recv()

            @pl.when(q != z)
            def _():
                c_cz(k, q, cmid.at[q, part(k)]).start()

    def stage_c3(k):
        @pl.when(home)
        def _():
            crecv[z, part(k)] = csend[r, part(k)]

        @pl.when(jnp.logical_not(home))
        def _():
            crecv[z, part(k)] = cmid[z, part(k)]

        for i in range(1, Z):
            q = (z + i) % Z
            ref = crecv.at[q, part(k)]
            remote(ref, ref, s_cz.at[k, 0], r_cz.at[k, q], r, sib).wait_recv()
        total = (crecv[0, part(k)].astype(F32) + crecv[1, part(k)].astype(F32)) + (
            crecv[2, part(k)].astype(F32) + crecv[3, part(k)].astype(F32)
        )
        out[part(k)] = (tok[part(k)].astype(F32) + total).astype(BF16)

    stages = {
        "send": stage_send, "st0": stage_st0, "st1": stage_st1, "st2": stage_st2, "a": stage_a, "m1": stage_m1,
        "b1": stage_b1, "b2": stage_b2, "b3": stage_b3, "b4": stage_b4, "c1": stage_c1, "c2": stage_c2, "c3": stage_c3,
    }
    for name, k in order:
        stages[name](k)

    for i in range(1, M):
        c_st(i).wait_send()
    for i in range(3):
        c_mi(i).wait_send()
    for k in range(K):
        for i in range(1, Z):
            c_a(k, i).wait_send()

        @pl.when(jnp.logical_not(home))
        def _():
            c_a(k, 0).wait_send()
            c_cz(k, r, csend.at[r, part(k)]).wait_send()

        for t in range(R):
            c_sib(k, t, xs.at[c, t, part(k)]).wait_send()
        for h in range(2):
            c_r1(k, h, 0).wait_send()
            c_r1(k, h, 1).wait_send()
            c_r2(k, h).wait_send()
            for i in range(3):
                c_ag(k, h, i).wait_send()
        c_os(k).wait_send()
        for i in range(3):
            c_cm(k, i).wait_send()
            q = peers[i]

            @pl.when(q != z)
            def _():
                c_cz(k, q, cmid.at[q, part(k)]).wait_send()


def schedule(K):
    seq = [("st0", 0), ("send", 0), ("st1", 0), ("send", 1), ("a", 0), ("st2", 0), ("send", 2), ("m1", 0), ("a", 1)]
    seq += [("send", k) for k in range(3, K)] + [("b1", 0)]
    for s in range(1, K + 4):
        for name, k in (
            ("m1", s), ("b2", s - 1), ("a", s + 1), ("b4", s - 2), ("b1", s), ("c2", s - 3), ("c1", s - 2),
            ("b3", s - 1), ("c3", s - 4),
        ):
            if 0 <= k < K:
                seq.append((name, k))
    return seq


def fused(tokens, norm_gain, hidden_bias, weight_in, weight_out, R, M, D, units):
    height, width = tokens.shape
    depth, ff = weight_in.shape
    half = ff // 2
    step = height // sum(units)
    cuts = [u * step for u in units]
    K = len(cuts)
    V = pltpu.VMEM
    S = pltpu.SemaphoreType.DMA
    vm = pl.BlockSpec(memory_space=pltpu.VMEM)
    hbm = pl.BlockSpec(memory_space=pltpu.HBM)
    return pl.pallas_call(
        functools.partial(kernel, R, M, D, cuts, schedule(K)),
        out_shape=jax.ShapeDtypeStruct(tokens.shape, BF16),
        in_specs=[vm, vm, vm, hbm, hbm],
        out_specs=vm,
        scratch_shapes=[
            V(weight_in.shape, BF16), V(weight_out.shape, BF16),
            V((2, R, height, width), BF16), V((2, R * max(cuts), width), BF16),
            V((M, 8, height), F32), V((R, 8, height), F32), V((R, height, 128), F32),
            V((2, R, height, half), BF16), V((2, 2, height, half), BF16), V((2, height, half), BF16),
            V((2, height, half), BF16), V((2, R, height, half), BF16),
            V((R, height, width), BF16), V((R, height, width), BF16), V((R, height, width), F32),
            V((R, height, width), BF16), V((R, height, width), BF16), V((R, height, width), BF16), S((2,)),
            S((K, R)), S((K, R)), S((K, R)), S((K, R)), S((M,)), S((M,)), S((3,)), S((R,)),
            S((K, 2, 2)), S((K, 2, 2)), S((K, 2)), S((K, 2)), S((K, 2, 3)), S((K, 2, R)), S((K,)), S((K,)),
            S((K, 3)), S((K, R)), S((K, R)), S((K, R)),
        ],
        compiler_params=pltpu.CompilerParams(
            collective_id=0, has_side_effects=True, vmem_limit_bytes=60 * 1024 * 1024
        ),
    )(tokens, norm_gain.reshape(M, 1, width), hidden_bias.reshape(1, ff), weight_in, weight_out)


def plain(tokens, norm_gain, hidden_bias, weight_in, weight_out, R, M, D):
    as_float = tokens.astype(F32)
    moment_sum, square_sum = lax.psum((jnp.sum(as_float, axis=1), jnp.sum(as_float * as_float, axis=1)), "mp")
    width = tokens.shape[1]
    gain = lax.dynamic_slice_in_dim(norm_gain, lax.axis_index("mp") * width, width)
    mean = moment_sum / D
    inverse = lax.rsqrt(jnp.maximum(square_sum / D - mean * mean, 0.0) + floor_value)
    part = ((as_float - mean[:, None]) * inverse[:, None] * gain[None, :]).astype(BF16)
    normed = lax.all_gather(part, "mp", axis=1, tiled=True)
    shuffled = lax.all_to_all(normed, "rows", split_axis=1, concat_axis=0, tiled=True)
    preact = lax.psum_scatter(
        jnp.dot(shuffled, weight_in, preferred_element_type=F32), "rows", scatter_dimension=0, tiled=True
    )
    hidden = jax.nn.gelu(preact + hidden_bias[None, :], approximate=False).astype(BF16)
    hidden = lax.all_gather(hidden, "rows", axis=0, tiled=True)
    terms = jnp.dot(hidden, weight_out, preferred_element_type=F32)
    terms = lax.all_to_all(terms, "rows", split_axis=0, concat_axis=1, tiled=True)
    branch = lax.psum_scatter(terms, "mp", scatter_dimension=1, tiled=True)
    return (as_float + branch).astype(BF16)


def solution(mesh):
    R, M = mesh.shape["rows"], mesh.shape["mp"]

    def body(tokens, norm_gain, hidden_bias, weight_in, weight_out):
        D = norm_gain.shape[0]
        aligned = tokens.shape[1] % 128 == 0 and weight_in.shape[1] % 512 == 0 and tokens.shape[0] == 16 * sum(UNITS)
        if R == 4 and M == 2 * R and aligned and tokens.shape[0] % 128 == 0:
            return fused(tokens, norm_gain, hidden_bias, weight_in, weight_out, R, M, D, UNITS)
        return plain(tokens, norm_gain, hidden_bias, weight_in, weight_out, R, M, D)

    return jax.shard_map(
        body,
        mesh=mesh,
        in_specs=(P("rows", "mp"), P(), P("mp"), P("rows", "mp"), P("mp", "rows")),
        out_specs=P("rows", "mp"),
        check_vma=False,
    )
```

time: 111 us -> 98.8 us (0.89)
  Pallas kernels: 110 us -> 96.7 us
    pallas_call x1, Pallas kernels: 110 us -> 96.7 us  [fused(): pl.pallas_call(functools.partial(kernel, R, M, D, cuts, schedule(K)), out...]
where the time goes in v1:
time: 98.8 us; the launch traced here: 98.3 us
  Pallas kernels  96.7 us (98%)
  local copies, waits for them, and re-layouts  1.62 us (2%)
    pallas_call x1, Pallas kernels, fused(): pl.pallas_call(functools.partial(kernel, R, M, D, cuts, schedule(K)), out...  96.7 us

profile of v1, /device:TPU:0, one launch (start us, length us, event | category | flops | bytes accessed | tf_op | source)
XLA Modules:
  0.0 98.3 jit_solution(16037232309440514596)
XLA Ops:
  0.0 96.7 %shard_map.55 = bf16[128,768]{1,0:T(8,128)(2,1)} custom-call(bf16[128,768]{1,0:T(8,128)(2,1)} %tok.1, f32[8,1,768]{2,1,0:T(1,128)} %bitcast.2, f32[1,3072]{1,0:T(1,128)} %bitcast.3, bf16[1536,3072]{1,0:T(8,128)(2,1)} %win_hbm.1, bf16[3072,1536]{1,0:T(8,128)(2,1)} %wout_hbm.1), custom_call_target="tpu_custom_call" | custom-call | tf_op jit(solution)/shard_map/pallas_call | solution.py:342
  96.7 1.6 %copy.7 = bf16[128,768]{1,0:T(8,128)(2,1)} copy(bf16[128,768]{1,0:T(8,128)(2,1)} %shard_map.55) | data formatting | bytes 393216

commit v2 on v1

--- a/solution.py
+++ b/solution.py
@@ -12,6 +12,8 @@
 BF16 = jnp.bfloat16
 floor_value = 0.1
 UNITS = (1, 2, 2, 2, 1)
+FAR_IN = (2, 3, 4)
+FAR_OUT = (0, 1)
 
 
 def gelu(x):
@@ -19,10 +21,10 @@
 
 
 def kernel(
-    R, M, D, cuts, order, tok, gain, bias, win_hbm, wout_hbm, out, win, wout, xs, nx, stc, mi, colst,
-    pbuf, r1, r2, qbuf, hid, osend, osib, oown, csend, cmid, crecv, wsem,
-    s_a, r_a, s_sib, r_sib, s_st, r_st, s_mi, r_mi, s_r1, r_r1, s_r2, r_r2, s_ag, r_ag, s_os, r_os,
-    s_cm, r_cm, s_cz, r_cz,
+    R, M, D, cuts, order, far_in, far_out, tok, gain, bias, win_hbm, wout_hbm, out, win, wout, xs, nx, stc, mi, colst,
+    pbuf, r1, r2, qbuf, hid, osend, osib, oown, csend, cmid, crecv, cfin, fin, wsem,
+    s_a, s_ap, s_af, s_ax, r_a, r_af, s_sib, r_sib, s_st, r_st, s_mi, r_mi, s_b, s_f, r_p, r_q, r_g, r_ag,
+    s_os, r_os, s_cm, s_cp, r_cm, s_cz, r_cz, s_fin, r_fin,
 ):
     r = lax.axis_index("rows")
     m = lax.axis_index("mp")
@@ -49,6 +51,12 @@
     def part(k):
         return pl.ds(offs[k], cuts[k])
 
+    def got(ref, sem):
+        remote(ref, ref, sem, sem, r, sib).wait_recv()
+
+    def sent(ref, sem):
+        remote(ref, ref, sem, sem, r, sib).wait_send()
+
     barrier = pltpu.get_barrier_semaphore()
 
     def greet(row, col):
@@ -76,48 +84,86 @@
 
     def c_a(k, i):
         zd = (z + i * toward + Z) % Z
-        return remote(tok.at[part(k)], xs.at[c, r, part(k)], s_a.at[k, i], r_a.at[k, r], z, 2 * zd + c)
+        return remote(tok.at[part(k)], xs.at[c, r, part(k)], (s_a if i else s_ap).at[0], r_a.at[k], z, 2 * zd + c)
 
     def c_sib(k, t, src):
-        return remote(src, xs.at[c, t, part(k)], s_sib.at[k, t], r_sib.at[k, t], r, sib)
+        return remote(src, xs.at[c, t, part(k)], s_sib.at[0], r_sib.at[k], r, sib)
 
     def c_st(i):
-        return remote(stc.at[m], stc.at[m], s_st.at[i], r_st.at[m], r, (m + i) % M)
+        return remote(stc.at[m], stc.at[m], s_st.at[0], r_st.at[0], r, (m + i) % M)
 
     def c_mi(i):
-        return remote(mi.at[r], mi.at[r], s_mi.at[i], r_mi.at[r], peers[i], m)
+        return remote(mi.at[r], mi.at[r], s_mi.at[0], r_mi.at[0], peers[i], m)
 
     def c_r1(k, h, i):
         tile = (first[h], rd)[i]
         return remote(
-            pbuf.at[h, tile, part(k)], r1.at[h, i, part(k)], s_r1.at[k, h, i], r_r1.at[k, h, i], first[h], m
+            pbuf.at[h, tile, part(k)], r1.at[h, i, part(k)], s_b.at[0], (r_q, r_p)[i].at[k, h], first[h], m
         )
 
     def c_r2(k, h):
-        return remote(qbuf.at[h, part(k)], r2.at[h, part(k)], s_r2.at[k, h], r_r2.at[k, h], second[h], m)
+        return remote(qbuf.at[h, part(k)], r2.at[h, part(k)], s_f.at[0], r_q.at[k, h], second[h], m)
 
     def c_ag(k, h, i):
         tile = (r, r, second[h])[i]
         to = (second[h], first[h], first[h])[i]
         ref = hid.at[h, tile, part(k)]
-        return remote(ref, ref, s_ag.at[k, h, i], r_ag.at[k, h, tile], to, m)
-
-    def w_ag(k, h, tile):
-        ref = hid.at[h, tile, part(k)]
-        return remote(ref, ref, s_ag.at[k, h, 0], r_ag.at[k, h, tile], first[h], m)
+        return remote(ref, ref, (s_b, s_b, s_f)[i].at[0], r_g.at[k, h] if i == 0 else r_ag.at[k], to, m)
 
     def c_os(k):
-        return remote(osend.at[:, part(k)], osib.at[:, part(k)], s_os.at[k], r_os.at[k], r, sib)
+        return remote(osend.at[:, part(k)], osib.at[:, part(k)], s_os.at[0], r_os.at[k], r, sib)
 
     def c_cm(k, i):
         t = peers[i]
-        return remote(csend.at[t, part(k)], cmid.at[r, part(k)], s_cm.at[k, i], r_cm.at[k, r], t, m)
+        return remote(csend.at[t, part(k)], cmid.at[r, part(k)], s_cm.at[0], r_cm.at[k], t, m)
 
     def c_cz(k, q, src):
-        return remote(src, crecv.at[z, part(k)], s_cz.at[k, q], r_cz.at[k, z], r, 2 * q + c)
+        return remote(src, crecv.at[z, part(k)], s_cz.at[0], r_cz.at[k], r, 2 * q + c)
+
+    def plane_of(k, t):
+        return (k + t) % Z
+
+    def tile_of(k):
+        return (z + Z * k - k) % Z
+
+    def c_ax(k, i, src):
+        t = tile_of(k)
+        zd = (z + i * toward + Z) % Z
+        return remote(src, xs.at[c, t, part(k)], s_ax.at[0], r_a.at[k], r, 2 * zd + c)
+
+    def c_a1(k):
+        return remote(
+            tok.at[part(k)], xs.at[c, r, part(k)], s_af.at[far_in.index(k)], r_af.at[far_in.index(k)], z,
+            2 * plane_of(k, r) + c,
+        )
+
+    def keeps(k):
+        return home & (plane_of(k, r) == z)
+
+    def c_cx(k, i):
+        zd = (z + i * toward + Z) % Z
+        t = (zd + Z * k - k) % Z
+        return remote(csend.at[t, part(k)], crecv.at[z, part(k)], s_cz.at[0], r_cz.at[k], r, 2 * zd + c)
+
+    def c_cp(k):
+        return remote(cfin.at[part(k)], cmid.at[r, part(k)], s_cp.at[far_out.index(k)], r_cm.at[k], tile_of(k), m)
+
+    def c_fin(k, q, src):
+        j = far_out.index(k)
+        return remote(src, fin.at[part(k)], s_fin.at[j], r_fin.at[j], r, 2 * q + c)
 
     def stage_send(k):
-        for i in range(1, Z):
+        if k in far_in:
+            @pl.when(keeps(k))
+            def _():
+                xs[c, r, part(k)] = tok[part(k)]
+
+            @pl.when(jnp.logical_not(keeps(k)))
+            def _():
+                c_a1(k).start()
+
+            return
+        for i in (1, 3, 2):
             c_a(k, i).start()
 
         @pl.when(home)
@@ -134,9 +180,7 @@
             c_st(i).start()
 
     def stage_st1(_):
-        for i in range(1, M):
-            q = (m + i) % M
-            remote(stc.at[q], stc.at[q], s_st.at[i], r_st.at[q], r, q).wait_recv()
+        got(stc.at[0:M - 1], r_st.at[0])
         tot = stc[0]
         for q in range(1, M):
             tot = tot + stc[q]
@@ -149,30 +193,54 @@
             c_mi(i).start()
 
     def stage_st2(_):
-        for i in range(3):
-            p = peers[i]
-            remote(mi.at[p], mi.at[p], s_mi.at[i], r_mi.at[p], p, m).wait_recv()
+        got(mi.at[0:R - 1], r_mi.at[0])
         sub = lax.broadcasted_iota(jnp.int32, (128, height), 0)
         for t in range(R):
             colst[t] = jnp.where(sub == 0, mi[t, 0:1], mi[t, 1:2]).T
 
+    def stage_a1(k):
+        if k not in far_in:
+            return
+        t = tile_of(k)
+
+        def spread(src):
+            for i in (1, 3, 2):
+                c_ax(k, i, src).start()
+            c_sib(k, t, src).start()
+
+        @pl.when(keeps(k))
+        def _():
+            spread(tok.at[part(k)])
+
+        @pl.when(jnp.logical_not(keeps(k)))
+        def _():
+            got(xs.at[c, t, part(k)], r_af.at[far_in.index(k)])
+            spread(xs.at[c, t, part(k)])
+
     def stage_a(k):
-        for i in range(R):
+        if k in far_in:
+            got(xs.at[c, 0:R - 1, part(k)], r_a.at[k])
+            for i in range(1, R):
+                t = (tile_of(k) + i) % R
+                c_sib(k, t, xs.at[c, t, part(k)]).start()
+            return
+
+        @pl.when(home)
+        def _():
+            got(xs.at[c, 0:R - 1, part(k)], r_a.at[k])
+
+        @pl.when(jnp.logical_not(home))
+        def _():
+            got(xs.at[c, :, part(k)], r_a.at[k])
+            c_sib(k, r, xs.at[c, r, part(k)]).start()
+
+        for i in range(1, R):
             t = (r + i) % R
-            if i == 0:
-                @pl.when(jnp.logical_not(home))
-                def _():
-                    remote(tok.at[part(k)], xs.at[c, r, part(k)], s_a.at[k, 0], r_a.at[k, r], r, sib).wait_recv()
-                    c_sib(k, r, xs.at[c, r, part(k)]).start()
-            else:
-                remote(tok.at[part(k)], xs.at[c, t, part(k)], s_a.at[k, 0], r_a.at[k, t], r, sib).wait_recv()
-                c_sib(k, t, xs.at[c, t, part(k)]).start()
+            c_sib(k, t, xs.at[c, t, part(k)]).start()
 
     def stage_m1(k):
         n = cuts[k]
-        for t in range(R):
-            ref = xs.at[1 - c, t, part(k)]
-            remote(ref, ref, s_sib.at[k, t], r_sib.at[k, t], r, sib).wait_recv()
+        got(xs.at[1 - c, :, part(k)], r_sib.at[k])
         stats = colst[:, part(k)].reshape(R * n, 128)
         mean_c, inv_c = stats[:, 0:1], stats[:, 1:2]
         for cc in range(2):
@@ -198,15 +266,14 @@
 
     def stage_b1(k):
         for h in range(2):
-            c_r1(k, h, 1).wait_recv()
+            got(r1.at[h, 1, part(k)], r_p.at[k, h])
             mine = pbuf[h, second[h], part(k)].astype(F32)
             qbuf[h, part(k)] = (mine + r1[h, 1, part(k)].astype(F32)).astype(BF16)
             c_r2(k, h).start()
 
     def stage_b2(k):
         for h in range(2):
-            c_r1(k, h, 0).wait_recv()
-            c_r2(k, h).wait_recv()
+            got(r1.at[h, :, part(k)], r_q.at[k, h])
             pre = pbuf[h, r, part(k)].astype(F32) + r1[h, 0, part(k)].astype(F32) + r2[h, part(k)].astype(F32)
             pre = pre + bias[0:1, h * half:(h + 1) * half]
             hid[h, r, part(k)] = gelu(pre).astype(BF16)
@@ -215,14 +282,12 @@
 
     def stage_b3(k):
         for h in range(2):
-            w_ag(k, h, second[h]).wait_recv()
+            got(hid.at[h, second[h], part(k)], r_g.at[k, h])
             c_ag(k, h, 2).start()
 
     def stage_b4(k):
         n = cuts[k]
-        for h in range(2):
-            w_ag(k, h, first[h]).wait_recv()
-            w_ag(k, h, rd).wait_recv()
+        got(hid.at[:, 0:2, part(k)], r_ag.at[k])
 
         if k == 0:
             pltpu.make_async_copy(wout_hbm, wout, wsem.at[1]).wait()
@@ -242,6 +307,13 @@
 
     def stage_c1(k):
         c_os(k).wait_recv()
+        if k in far_out:
+            t = tile_of(k)
+            csend[:, part(k)] = (oown[:, part(k)] + osib[:, part(k)].astype(F32)).astype(BF16)
+            for i in (1, 3, 2):
+                c_cx(k, i).start()
+            oown[t, part(k)] = oown[t, part(k)] + osib[t, part(k)].astype(F32)
+            return
         csend[:, part(k)] = (oown[:, part(k)] + osib[:, part(k)].astype(F32)).astype(BF16)
         for i in range(3):
             c_cm(k, i).start()
@@ -251,15 +323,65 @@
             c_cz(k, r, csend.at[r, part(k)]).start()
 
     def stage_c2(k):
-        for i in (1, 2, 0):
+        if k in far_out:
+            t = tile_of(k)
+            total = oown[t, part(k)]
+            got(crecv.at[0:Z - 1, part(k)], r_cz.at[k])
+            for i in range(1, Z):
+                q = (z + i) % Z
+                total = total + crecv[q, part(k)].astype(F32)
+            cfin[part(k)] = total.astype(BF16)
+
+            @pl.when(t != r)
+            def _():
+                c_cp(k).start()
+
+            return
+        got(cmid.at[0:R - 1, part(k)], r_cm.at[k])
+        for i in range(3):
             q = peers[i]
-            remote(csend.at[r, part(k)], cmid.at[q, part(k)], s_cm.at[k, i], r_cm.at[k, q], q, m).wait_recv()
 
             @pl.when(q != z)
             def _():
                 c_cz(k, q, cmid.at[q, part(k)]).start()
 
+    def stage_c4(k):
+        if k not in far_out:
+            return
+
+        @pl.when(tile_of(k) == r)
+        def _():
+            @pl.when(jnp.logical_not(home))
+            def _():
+                c_fin(k, r, cfin.at[part(k)]).start()
+
+            got(cmid.at[0:R - 1, part(k)], r_cm.at[k])
+            for i in range(3):
+                q = peers[i]
+
+                @pl.when(q != z)
+                def _():
+                    c_fin(k, q, cmid.at[q, part(k)]).start()
+
     def stage_c3(k):
+        if k in far_out:
+            mine = tile_of(k) == r
+
+            @pl.when(mine & home)
+            def _():
+                fin[part(k)] = cfin[part(k)]
+
+            @pl.when(mine & jnp.logical_not(home))
+            def _():
+                fin[part(k)] = cmid[z, part(k)]
+
+            @pl.when(jnp.logical_not(mine))
+            def _():
+                got(fin.at[part(k)], r_fin.at[far_out.index(k)])
+
+            out[part(k)] = (tok[part(k)].astype(F32) + fin[part(k)].astype(F32)).astype(BF16)
+            return
+
         @pl.when(home)
         def _():
             crecv[z, part(k)] = csend[r, part(k)]
@@ -268,64 +390,81 @@
         def _():
             crecv[z, part(k)] = cmid[z, part(k)]
 
-        for i in range(1, Z):
-            q = (z + i) % Z
-            ref = crecv.at[q, part(k)]
-            remote(ref, ref, s_cz.at[k, 0], r_cz.at[k, q], r, sib).wait_recv()
+        got(crecv.at[0:Z - 1, part(k)], r_cz.at[k])
         total = (crecv[0, part(k)].astype(F32) + crecv[1, part(k)].astype(F32)) + (
             crecv[2, part(k)].astype(F32) + crecv[3, part(k)].astype(F32)
         )
         out[part(k)] = (tok[part(k)].astype(F32) + total).astype(BF16)
 
+    def stage_e(_):
+        near = sum(cuts[k] for k in range(K) if k not in far_in)
+        sent(xs.at[0, 0:Z - 1, 0:near], s_a.at[0])
+        sent(xs.at[0, 0:Z - 1, near:height], s_ax.at[0])
+
+        @pl.when(jnp.logical_not(home))
+        def _():
+            sent(tok.at[0:near], s_ap.at[0])
+
+        for k in far_in:
+            @pl.when(jnp.logical_not(keeps(k)))
+            def _():
+                c_a1(k).wait_send()
+
+        sent(xs.at[0], s_sib.at[0])
+        sent(stc.at[0:M - 1], s_st.at[0])
+        sent(mi.at[0:R - 1], s_mi.at[0])
+        sent(hid, s_b.at[0])
+        sent(hid.at[:, 0:2], s_f.at[0])
+        sent(osend, s_os.at[0])
+        sent(csend.at[0:R - 1, 0:sum(cuts[k] for k in range(K) if k not in far_out)], s_cm.at[0])
+        for k in far_out:
+            @pl.when(tile_of(k) != r)
+            def _():
+                c_cp(k).wait_send()
+
+            @pl.when(tile_of(k) == r)
+            def _():
+                sent(crecv.at[0:Z - 1, part(k)], s_fin.at[far_out.index(k)])
+
+        sent(crecv.at[0:Z - 1], s_cz.at[0])
+
     stages = {
-        "send": stage_send, "st0": stage_st0, "st1": stage_st1, "st2": stage_st2, "a": stage_a, "m1": stage_m1,
-        "b1": stage_b1, "b2": stage_b2, "b3": stage_b3, "b4": stage_b4, "c1": stage_c1, "c2": stage_c2, "c3": stage_c3,
+        "send": stage_send, "st0": stage_st0, "st1": stage_st1, "st2": stage_st2, "a1": stage_a1, "a": stage_a,
+        "m1": stage_m1, "b1": stage_b1, "b2": stage_b2, "b3": stage_b3, "b4": stage_b4, "c1": stage_c1,
+        "c2": stage_c2, "c4": stage_c4, "c3": stage_c3, "e": stage_e,
     }
+    assert len(set(order)) == len(order)
     for name, k in order:
         stages[name](k)
 
-    for i in range(1, M):
-        c_st(i).wait_send()
-    for i in range(3):
-        c_mi(i).wait_send()
-    for k in range(K):
-        for i in range(1, Z):
-            c_a(k, i).wait_send()
-
-        @pl.when(jnp.logical_not(home))
-        def _():
-            c_a(k, 0).wait_send()
-            c_cz(k, r, csend.at[r, part(k)]).wait_send()
-
-        for t in range(R):
-            c_sib(k, t, xs.at[c, t, part(k)]).wait_send()
-        for h in range(2):
-            c_r1(k, h, 0).wait_send()
-            c_r1(k, h, 1).wait_send()
-            c_r2(k, h).wait_send()
-            for i in range(3):
-                c_ag(k, h, i).wait_send()
-        c_os(k).wait_send()
-        for i in range(3):
-            c_cm(k, i).wait_send()
-            q = peers[i]
-
-            @pl.when(q != z)
-            def _():
-                c_cz(k, q, cmid.at[q, part(k)]).wait_send()
+
+ORDER = (
+    "st0_0 send_0 send_1",
+    "send_2 send_3 send_4",
+    "st1_0 a_0 st2_0",
+    "m1_0 a_1 m1_1",
+    "a1_2 b1_0 a1_3",
+    "b1_1 b2_0 a_2",
+    "b2_1 a1_4 m1_2",
+    "b3_0 a_3 b3_1",
+    "b1_2 a_4 m1_3",
+    "b4_0 m1_4 b1_3",
+    "b4_1 b2_2 c1_1",
+    "b2_3 c1_0 b1_4",
+    "b3_2 c2_1 b3_3",
+    "c2_0 b2_4 b4_2",
+    "c1_2 b4_3 c4_1",
+    "b3_4 c1_3 c4_0",
+    "c2_2 b4_4 c1_4",
+    "c3_0 c2_3 c2_4",
+    "c3_1 c3_2 c3_3",
+    "c3_4 e_0",
+)
 
 
 def schedule(K):
-    seq = [("st0", 0), ("send", 0), ("st1", 0), ("send", 1), ("a", 0), ("st2", 0), ("send", 2), ("m1", 0), ("a", 1)]
-    seq += [("send", k) for k in range(3, K)] + [("b1", 0)]
-    for s in range(1, K + 4):
-        for name, k in (
-            ("m1", s), ("b2", s - 1), ("a", s + 1), ("b4", s - 2), ("b1", s), ("c2", s - 3), ("c1", s - 2),
-            ("b3", s - 1), ("c3", s - 4),
-        ):
-            if 0 <= k < K:
-                seq.append((name, k))
-    return seq
+    names = " ".join(ORDER).split()
+    return [(name.split("_")[0], int(name.split("_")[1])) for name in names]
 
 
 def fused(tokens, norm_gain, hidden_bias, weight_in, weight_out, R, M, D, units):
@@ -340,7 +479,7 @@
     vm = pl.BlockSpec(memory_space=pltpu.VMEM)
     hbm = pl.BlockSpec(memory_space=pltpu.HBM)
     return pl.pallas_call(
-        functools.partial(kernel, R, M, D, cuts, schedule(K)),
+        functools.partial(kernel, R, M, D, cuts, schedule(K), FAR_IN, FAR_OUT),
         out_shape=jax.ShapeDtypeStruct(tokens.shape, BF16),
         in_specs=[vm, vm, vm, hbm, hbm],
         out_specs=vm,
@@ -351,10 +490,11 @@
             V((2, R, height, half), BF16), V((2, 2, height, half), BF16), V((2, height, half), BF16),
             V((2, height, half), BF16), V((2, R, height, half), BF16),
             V((R, height, width), BF16), V((R, height, width), BF16), V((R, height, width), F32),
-            V((R, height, width), BF16), V((R, height, width), BF16), V((R, height, width), BF16), S((2,)),
-            S((K, R)), S((K, R)), S((K, R)), S((K, R)), S((M,)), S((M,)), S((3,)), S((R,)),
-            S((K, 2, 2)), S((K, 2, 2)), S((K, 2)), S((K, 2)), S((K, 2, 3)), S((K, 2, R)), S((K,)), S((K,)),
-            S((K, 3)), S((K, R)), S((K, R)), S((K, R)),
+            V((R, height, width), BF16), V((R, height, width), BF16), V((R, height, width), BF16),
+            V((height, width), BF16), V((height, width), BF16), S((2,)),
+            S((1,)), S((1,)), S((len(FAR_IN),)), S((1,)), S((K,)), S((len(FAR_IN),)), S((1,)), S((K,)), S((1,)), S((1,)),
+            S((1,)), S((1,)), S((1,)), S((1,)), S((K, 2)), S((K, 2)), S((K, 2)), S((K,)),
+            S((1,)), S((K,)), S((1,)), S((len(FAR_OUT),)), S((K,)), S((1,)), S((K,)), S((len(FAR_OUT),)), S((len(FAR_OUT),)),
         ],
         compiler_params=pltpu.CompilerParams(
             collective_id=0, has_side_effects=True, vmem_limit_bytes=60 * 1024 * 1024

time: 98.8 us -> 88.9 us (0.90)
  Pallas kernels: 96.7 us -> 86 us
    pallas_call x1, Pallas kernels: 96.7 us -> 86 us  [fused(): pl.pallas_call(functools.partial(kernel, R, M, D, cuts, schedule(K), FAR_...]
where the time goes in v2:
time: 88.9 us; the launch traced here: 87.6 us
  Pallas kernels  86 us (97%)
  local copies, waits for them, and re-layouts  1.62 us (2%)
    pallas_call x1, Pallas kernels, fused(): pl.pallas_call(functools.partial(kernel, R, M, D, cuts, schedule(K), FAR_...  86 us

profile of v2, /device:TPU:0, one launch (start us, length us, event | category | flops | bytes accessed | tf_op | source)
XLA Modules:
  0.0 87.6 jit_solution(7469968241368708027)
XLA Ops:
  0.0 86.0 %shard_map.55 = bf16[128,768]{1,0:T(8,128)(2,1)} custom-call(bf16[128,768]{1,0:T(8,128)(2,1)} %tok.1, f32[8,1,768]{2,1,0:T(1,128)} %bitcast.2, f32[1,3072]{1,0:T(1,128)} %bitcast.3, bf16[1536,3072]{1,0:T(8,128)(2,1)} %win_hbm.1, bf16[3072,1536]{1,0:T(8,128)(2,1)} %wout_hbm.1), custom_call_target="tpu_custom_call" | custom-call | tf_op jit(solution)/shard_map/pallas_call | solution.py:481
  86.0 1.6 %copy.7 = bf16[128,768]{1,0:T(8,128)(2,1)} copy(bf16[128,768]{1,0:T(8,128)(2,1)} %shard_map.55) | data formatting | bytes 393216

commit v3 on v2

v3 whole, which is shorter than its diff:
```python
import functools

import jax
import jax.numpy as jnp
from jax import lax
from jax.experimental import pallas as pl
from jax.experimental.pallas import tpu as pltpu
from jax.sharding import PartitionSpec as P

MESH = pl.DeviceIdType.MESH
F32 = jnp.float32
BF16 = jnp.bfloat16
floor_value = 0.1
UNITS = ((1,), (2,), (2,), (1,), (1,), (1,))
FAR_IN = (2, 3, 4, 5)
FAR_OUT = (0, 1, 2, 3)


def gelu(x):
    return 0.5 * x * (1.0 + lax.erf(x * 0.7071067811865476))


def kernel(
    R, M, D, groups, order, far_in, far_out, tok_hbm, gain_hbm, bias_hbm, win_hbm, wout_hbm, out, tok, gain, bias,
    win, wout, xs, nx, stc, mi, colst,
    pbuf, r1, r2, qbuf, hid, osend, osib, oown, csend, cmid, crecv, cfin, fin, wsem,
    s_a, s_ap, s_af, s_ax, r_a, r_af, s_sib, r_sib, s_st, r_st, s_mi, r_mi, s_b, s_f, r_p, r_q, r_g, r_ag,
    s_os, r_os, s_cm, s_cp, r_cm, s_cz, r_cz, s_fin, r_fin,
):
    r = lax.axis_index("rows")
    m = lax.axis_index("mp")
    Z = M // 2
    z, c = m // 2, m % 2
    sib = 2 * z + 1 - c
    height, width = tok.shape
    cuts = [n for group in groups for n in group]
    wide = [sum(group) for group in groups]
    firsts = [sum(len(group) for group in groups[:g]) for g in range(len(groups))]
    subs = [range(firsts[g], firsts[g] + len(groups[g])) for g in range(len(groups))]
    G = len(groups)
    half = win.shape[1] // 2
    K = len(cuts)
    offs = [sum(cuts[:k]) for k in range(K)]
    rx, ry, rd = r + 1 - 2 * (r % 2), (r + 2) % 4, 3 - r
    first, second = (rx, ry), (ry, rx)
    peers = (rd, rx, ry)
    home = z == r

    in_tok = pltpu.make_async_copy(tok_hbm, tok, wsem.at[2])
    in_gain = pltpu.make_async_copy(gain_hbm, gain, wsem.at[3])
    in_bias = pltpu.make_async_copy(bias_hbm, bias, wsem.at[4])
    in_tok.start()

    def remote(src, dst, ssem, rsem, row, col):
        return pltpu.make_async_remote_copy(
            src_ref=src, dst_ref=dst, send_sem=ssem, recv_sem=rsem, device_id=(row, col), device_id_type=MESH
        )

    def part(k):
        return pl.ds(offs[k], cuts[k])

    def span(g):
        return pl.ds(offs[firsts[g]], wide[g])

    def got(ref, sem):
        remote(ref, ref, sem, sem, r, sib).wait_recv()

    def sent(ref, sem):
        remote(ref, ref, sem, sem, r, sib).wait_send()

    barrier = pltpu.get_barrier_semaphore()

    def greet(row, col):
        pl.semaphore_signal(barrier, inc=1, device_id=(row, col), device_id_type=MESH)

    for i in range(1, M):
        greet(r, (m + i) % M)
    for i in range(1, R):
        greet((r + i) % R, m)

    @pl.when(jnp.logical_not(home))
    def _():
        for i in range(1, R):
            greet((r + i) % R, 2 * r + c)

    in_gain.start()
    in_bias.start()
    pltpu.make_async_copy(win_hbm, win, wsem.at[0]).start()
    pltpu.make_async_copy(wout_hbm, wout, wsem.at[1]).start()
    in_tok.wait()
    own = tok[...].astype(F32)
    lane = lax.broadcasted_iota(jnp.int32, (height, 128), 1)
    s1 = jnp.sum(own, axis=1, keepdims=True)
    s2 = jnp.sum(own * own, axis=1, keepdims=True)
    stc[m] = jnp.where(lane == 0, s1, s2).T[0:8]

    pl.semaphore_wait(barrier, (M - 1) + (R - 1) + jnp.where(home, 0, R - 1))

    toward = 2 * (z // 2) - 1

    def c_a(k, i):
        zd = (z + i * toward + Z) % Z
        return remote(tok.at[span(k)], xs.at[c, r, span(k)], (s_a if i else s_ap).at[0], r_a.at[k], z, 2 * zd + c)

    def c_sib(k, t, src):
        return remote(src, xs.at[c, t, span(k)], s_sib.at[0], r_sib.at[k], r, sib)

    def c_st(i):
        return remote(stc.at[m], stc.at[m], s_st.at[0], r_st.at[0], r, (m + i) % M)

    def c_mi(i):
        return remote(mi.at[r], mi.at[r], s_mi.at[0], r_mi.at[0], peers[i], m)

    def c_r1(k, h, i):
        tile = (first[h], rd)[i]
        return remote(
            pbuf.at[h, tile, part(k)], r1.at[h, i, part(k)], s_b.at[0], (r_q, r_p)[i].at[k, h], first[h], m
        )

    def c_r2(k, h):
        return remote(qbuf.at[h, part(k)], r2.at[h, part(k)], s_f.at[0], r_q.at[k, h], second[h], m)

    def c_ag(k, h, i):
        tile = (r, r, second[h])[i]
        to = (second[h], first[h], first[h])[i]
        ref = hid.at[h, tile, part(k)]
        return remote(ref, ref, (s_b, s_b, s_f)[i].at[0], r_g.at[k, h] if i == 0 else r_ag.at[k], to, m)

    def c_os(k):
        return remote(osend.at[:, span(k)], osib.at[:, span(k)], s_os.at[0], r_os.at[k], r, sib)

    def c_cm(k, i):
        t = peers[i]
        return remote(csend.at[t, span(k)], cmid.at[r, span(k)], s_cm.at[0], r_cm.at[k], t, m)

    def c_cz(k, q, src):
        return remote(src, crecv.at[z, span(k)], s_cz.at[0], r_cz.at[k], r, 2 * q + c)

    def plane_of(k, t):
        return (k + t) % Z

    def tile_of(k):
        return (z + Z * k - k) % Z

    def c_ax(k, i, src):
        t = tile_of(k)
        zd = (z + i * toward + Z) % Z
        return remote(src, xs.at[c, t, span(k)], s_ax.at[0], r_a.at[k], r, 2 * zd + c)

    def c_a1(k):
        return remote(
            tok.at[span(k)], xs.at[c, r, span(k)], s_af.at[far_in.index(k)], r_af.at[far_in.index(k)], z,
            2 * plane_of(k, r) + c,
        )

    def keeps(k):
        return home & (plane_of(k, r) == z)

    def c_cx(k, i):
        zd = (z + i * toward + Z) % Z
        t = (zd + Z * k - k) % Z
        return remote(csend.at[t, span(k)], crecv.at[z, span(k)], s_cz.at[0], r_cz.at[k], r, 2 * zd + c)

    def c_cp(k):
        return remote(cfin.at[span(k)], cmid.at[r, span(k)], s_cp.at[far_out.index(k)], r_cm.at[k], tile_of(k), m)

    def c_fin(k, q, src):
        j = far_out.index(k)
        return remote(src, fin.at[span(k)], s_fin.at[j], r_fin.at[j], r, 2 * q + c)

    def stage_send(k):
        if k in far_in:
            @pl.when(keeps(k))
            def _():
                xs[c, r, span(k)] = tok[span(k)]

            @pl.when(jnp.logical_not(keeps(k)))
            def _():
                c_a1(k).start()

            return
        for i in (1, 3, 2):
            c_a(k, i).start()

        @pl.when(home)
        def _():
            xs[c, r, span(k)] = tok[span(k)]
            c_sib(k, r, tok.at[span(k)]).start()

        @pl.when(jnp.logical_not(home))
        def _():
            c_a(k, 0).start()

    def stage_st0(_):
        for i in range(1, M):
            c_st(i).start()

    def stage_st1(_):
        got(stc.at[0:M - 1], r_st.at[0])
        tot = stc[0]
        for q in range(1, M):
            tot = tot + stc[q]
        mean = tot[0:1] / D
        var = jnp.maximum(tot[1:2] / D - mean * mean, 0.0)
        inv = lax.rsqrt(var + floor_value)
        sub = lax.broadcasted_iota(jnp.int32, (8, height), 0)
        mi[r] = jnp.where(sub == 0, mean, inv)
        for i in range(3):
            c_mi(i).start()

    def stage_st2(_):
        got(mi.at[0:R - 1], r_mi.at[0])
        sub = lax.broadcasted_iota(jnp.int32, (128, height), 0)
        for t in range(R):
            colst[t] = jnp.where(sub == 0, mi[t, 0:1], mi[t, 1:2]).T

    def stage_a1(k):
        if k not in far_in:
            return
        t = tile_of(k)

        def spread(src):
            for i in (1, 3, 2):
                c_ax(k, i, src).start()
            c_sib(k, t, src).start()

        @pl.when(keeps(k))
        def _():
            spread(tok.at[span(k)])

        @pl.when(jnp.logical_not(keeps(k)))
        def _():
            got(xs.at[c, t, span(k)], r_af.at[far_in.index(k)])
            spread(xs.at[c, t, span(k)])

    def stage_a(k):
        if k in far_in:
            got(xs.at[c, 0:R - 1, span(k)], r_a.at[k])
            for i in range(1, R):
                t = (tile_of(k) + i) % R
                c_sib(k, t, xs.at[c, t, span(k)]).start()
            return

        @pl.when(home)
        def _():
            got(xs.at[c, 0:R - 1, span(k)], r_a.at[k])

        @pl.when(jnp.logical_not(home))
        def _():
            got(xs.at[c, :, span(k)], r_a.at[k])
            c_sib(k, r, xs.at[c, r, span(k)]).start()

        for i in range(1, R):
            t = (r + i) % R
            c_sib(k, t, xs.at[c, t, span(k)]).start()

    def stage_m1(k):
        n = wide[k]
        got(xs.at[1 - c, :, span(k)], r_sib.at[k])
        if k == 0:
            in_gain.wait()
        stats = colst[:, span(k)].reshape(R * n, 128)
        mean_c, inv_c = stats[:, 0:1], stats[:, 1:2]
        for cc in range(2):
            x = xs[cc, :, span(k)].astype(F32).reshape(R * n, width)
            nx[cc, 0:R * n] = ((x - mean_c) * inv_c * gain[2 * r + cc]).astype(BF16)

        if k == 0:
            pltpu.make_async_copy(win_hbm, win, wsem.at[0]).wait()
            in_bias.wait()

        tile = half // 2
        for h in range(2):
            def col(j, _):
                at = pl.multiple_of(j * tile, 128)
                wat = pl.multiple_of(h * half + j * tile, 128)
                acc = jnp.dot(nx[0, 0:R * n], win[0:width, pl.ds(wat, tile)], preferred_element_type=F32)
                acc += jnp.dot(nx[1, 0:R * n], win[width:2 * width, pl.ds(wat, tile)], preferred_element_type=F32)
                pbuf[h, :, span(k), pl.ds(at, tile)] = acc.astype(BF16).reshape(R, n, tile)
                return 0

            lax.fori_loop(0, 2, col, 0)
            for sub in subs[k]:
                c_r1(sub, h, 1).start()
                c_r1(sub, h, 0).start()

    def stage_b1(k):
        for h in range(2):
            got(r1.at[h, 1, part(k)], r_p.at[k, h])
            mine = pbuf[h, second[h], part(k)].astype(F32)
            qbuf[h, part(k)] = (mine + r1[h, 1, part(k)].astype(F32)).astype(BF16)
            c_r2(k, h).start()

    def stage_b2(k):
        for h in range(2):
            got(r1.at[h, :, part(k)], r_q.at[k, h])
            pre = pbuf[h, r, part(k)].astype(F32) + r1[h, 0, part(k)].astype(F32) + r2[h, part(k)].astype(F32)
            pre = pre + bias[0:1, h * half:(h + 1) * half]
            hid[h, r, part(k)] = gelu(pre).astype(BF16)
            c_ag(k, h, 0).start()
            c_ag(k, h, 1).start()

    def stage_b3(k):
        for h in range(2):
            got(hid.at[h, second[h], part(k)], r_g.at[k, h])
            c_ag(k, h, 2).start()

    def stage_b4(k):
        n = wide[k]
        for sub in subs[k]:
            got(hid.at[:, 0:2, part(sub)], r_ag.at[sub])

        if k == 0:
            pltpu.make_async_copy(wout_hbm, wout, wsem.at[1]).wait()

        def product(cc):
            at = pl.multiple_of(cc * width, 128)
            acc = None
            for h in range(2):
                a = hid[h, :, span(k)].reshape(R * n, half)
                term = jnp.dot(a, wout[h * half:(h + 1) * half, pl.ds(at, width)], preferred_element_type=F32)
                acc = term if acc is None else acc + term
            return acc.reshape(R, n, width)

        osend[:, span(k)] = product(1 - c).astype(BF16)
        c_os(k).start()
        oown[:, span(k)] = product(c)

    def stage_c1(k):
        c_os(k).wait_recv()
        if k in far_out:
            t = tile_of(k)
            csend[:, span(k)] = (oown[:, span(k)] + osib[:, span(k)].astype(F32)).astype(BF16)
            for i in (1, 3, 2):
                c_cx(k, i).start()
            oown[t, span(k)] = oown[t, span(k)] + osib[t, span(k)].astype(F32)
            return
        csend[:, span(k)] = (oown[:, span(k)] + osib[:, span(k)].astype(F32)).astype(BF16)
        for i in range(3):
            c_cm(k, i).start()

        @pl.when(jnp.logical_not(home))
        def _():
            c_cz(k, r, csend.at[r, span(k)]).start()

    def stage_c2(k):
        if k in far_out:
            t = tile_of(k)
            total = oown[t, span(k)]
            got(crecv.at[0:Z - 1, span(k)], r_cz.at[k])
            for i in range(1, Z):
                q = (z + i) % Z
                total = total + crecv[q, span(k)].astype(F32)
            cfin[span(k)] = total.astype(BF16)

            @pl.when(t != r)
            def _():
                c_cp(k).start()

            return
        got(cmid.at[0:R - 1, span(k)], r_cm.at[k])
        for i in range(3):
            q = peers[i]

            @pl.when(q != z)
            def _():
                c_cz(k, q, cmid.at[q, span(k)]).start()

    def stage_c4(k):
        if k not in far_out:
            return

        @pl.when(tile_of(k) == r)
        def _():
            @pl.when(jnp.logical_not(home))
            def _():
                c_fin(k, r, cfin.at[span(k)]).start()

            got(cmid.at[0:R - 1, span(k)], r_cm.at[k])
            for i in range(3):
                q = peers[i]

                @pl.when(q != z)
                def _():
                    c_fin(k, q, cmid.at[q, span(k)]).start()

    def stage_c3(k):
        if k in far_out:
            mine = tile_of(k) == r

            @pl.when(mine & home)
            def _():
                fin[span(k)] = cfin[span(k)]

            @pl.when(mine & jnp.logical_not(home))
            def _():
                fin[span(k)] = cmid[z, span(k)]

            @pl.when(jnp.logical_not(mine))
            def _():
                got(fin.at[span(k)], r_fin.at[far_out.index(k)])

            out[span(k)] = (tok[span(k)].astype(F32) + fin[span(k)].astype(F32)).astype(BF16)
            return

        @pl.when(home)
        def _():
            crecv[z, span(k)] = csend[r, span(k)]

        @pl.when(jnp.logical_not(home))
        def _():
            crecv[z, span(k)] = cmid[z, span(k)]

        got(crecv.at[0:Z - 1, span(k)], r_cz.at[k])
        total = (crecv[0, span(k)].astype(F32) + crecv[1, span(k)].astype(F32)) + (
            crecv[2, span(k)].astype(F32) + crecv[3, span(k)].astype(F32)
        )
        out[span(k)] = (tok[span(k)].astype(F32) + total).astype(BF16)

    def stage_e(_):
        near = sum(wide[k] for k in range(G) if k not in far_in)
        sent(xs.at[0, 0:Z - 1, 0:near], s_a.at[0])
        sent(xs.at[0, 0:Z - 1, near:height], s_ax.at[0])

        @pl.when(jnp.logical_not(home))
        def _():
            sent(tok.at[0:near], s_ap.at[0])

        for k in far_in:
            @pl.when(jnp.logical_not(keeps(k)))
            def _():
                c_a1(k).wait_send()

        sent(xs.at[0], s_sib.at[0])
        sent(stc.at[0:M - 1], s_st.at[0])
        sent(mi.at[0:R - 1], s_mi.at[0])
        sent(hid, s_b.at[0])
        sent(hid.at[:, 0:2], s_f.at[0])
        sent(osend, s_os.at[0])
        sent(csend.at[0:R - 1, 0:sum(wide[k] for k in range(G) if k not in far_out)], s_cm.at[0])
        for k in far_out:
            @pl.when(tile_of(k) != r)
            def _():
                c_cp(k).wait_send()

            @pl.when(tile_of(k) == r)
            def _():
                sent(crecv.at[0:Z - 1, span(k)], s_fin.at[far_out.index(k)])

        sent(crecv.at[0:Z - 1], s_cz.at[0])

    stages = {
        "send": stage_send, "st0": stage_st0, "st1": stage_st1, "st2": stage_st2, "a1": stage_a1, "a": stage_a,
        "m1": stage_m1, "b1": stage_b1, "b2": stage_b2, "b3": stage_b3, "b4": stage_b4, "c1": stage_c1,
        "c2": stage_c2, "c4": stage_c4, "c3": stage_c3, "e": stage_e,
    }
    assert len(set(order)) == len(order)
    for name, k in order:
        stages[name](k)


ORDER = (
    "st0_0 send_0 send_1",
    "send_2 send_3 send_4",
    "send_5 st1_0 a_0",
    "st2_0 m1_0 a_1",
    "m1_1 b1_0 a1_2",
    "a1_5 b1_1 b2_0",
    "b2_1 a1_4 a_2",
    "a1_3 m1_2 b3_0",
    "b1_2 a_3 b3_1",
    "m1_3 b2_2 a_4",
    "b4_0 b1_3 m1_4",
    "b4_1 c1_1 c1_0",
    "b3_2 a_5 b2_3",
    "m1_5 b1_4 b4_2",
    "b3_3 c1_2 b1_5",
    "b2_4 b2_5 b4_3",
    "b3_4 c2_1 c1_3",
    "c2_0 c2_2 b3_5",
    "b4_4 c1_4 c2_3",
    "c4_0 c4_1 b4_5",
    "c4_2 c1_5 c2_4",
    "c4_3 c2_5 c3_0",
    "c3_3 c3_2 c3_4",
    "c3_1 c3_5 e_0",
)


def schedule():
    names = " ".join(ORDER).split()
    return [(name.split("_")[0], int(name.split("_")[1])) for name in names]


def fused(tokens, norm_gain, hidden_bias, weight_in, weight_out, R, M, D):
    height, width = tokens.shape
    depth, ff = weight_in.shape
    half = ff // 2
    step = height // sum(sum(group) for group in UNITS)
    groups = [[u * step for u in group] for group in UNITS]
    K, G = sum(len(group) for group in groups), len(groups)
    V = pltpu.VMEM
    S = pltpu.SemaphoreType.DMA
    vm = pl.BlockSpec(memory_space=pltpu.VMEM)
    hbm = pl.BlockSpec(memory_space=pltpu.HBM)
    return pl.pallas_call(
        functools.partial(kernel, R, M, D, groups, schedule(), FAR_IN, FAR_OUT),
        out_shape=pltpu.VMEM(tokens.shape, BF16),
        in_specs=[hbm, hbm, hbm, hbm, hbm],
        out_specs=vm,
        scratch_shapes=[
            V(tokens.shape, BF16), V((M, 1, width), F32), V((1, ff), F32), V(weight_in.shape, BF16), V(weight_out.shape, BF16),
            V((2, R, height, width), BF16), V((2, R * max(sum(group) for group in groups), width), BF16),
            V((M, 8, height), F32), V((R, 8, height), F32), V((R, height, 128), F32),
            V((2, R, height, half), BF16), V((2, 2, height, half), BF16), V((2, height, half), BF16),
            V((2, height, half), BF16), V((2, R, height, half), BF16),
            V((R, height, width), BF16), V((R, height, width), BF16), V((R, height, width), F32),
            V((R, height, width), BF16), V((R, height, width), BF16), V((R, height, width), BF16),
            V((height, width), BF16), V((height, width), BF16), S((5,)),
            S((1,)), S((1,)), S((len(FAR_IN),)), S((1,)), S((G,)), S((len(FAR_IN),)), S((1,)), S((G,)), S((1,)), S((1,)),
            S((1,)), S((1,)), S((1,)), S((1,)), S((K, 2)), S((K, 2)), S((K, 2)), S((K,)),
            S((1,)), S((G,)), S((1,)), S((len(FAR_OUT),)), S((G,)), S((1,)), S((G,)), S((len(FAR_OUT),)), S((len(FAR_OUT),)),
        ],
        compiler_params=pltpu.CompilerParams(
            collective_id=0, has_side_effects=True, vmem_limit_bytes=60 * 1024 * 1024
        ),
    )(tokens, norm_gain.reshape(M, 1, width), hidden_bias.reshape(1, ff), weight_in, weight_out)


def plain(tokens, norm_gain, hidden_bias, weight_in, weight_out, R, M, D):
    as_float = tokens.astype(F32)
    moment_sum, square_sum = lax.psum((jnp.sum(as_float, axis=1), jnp.sum(as_float * as_float, axis=1)), "mp")
    width = tokens.shape[1]
    gain = lax.dynamic_slice_in_dim(norm_gain, lax.axis_index("mp") * width, width)
    mean = moment_sum / D
    inverse = lax.rsqrt(jnp.maximum(square_sum / D - mean * mean, 0.0) + floor_value)
    part = ((as_float - mean[:, None]) * inverse[:, None] * gain[None, :]).astype(BF16)
    normed = lax.all_gather(part, "mp", axis=1, tiled=True)
    shuffled = lax.all_to_all(normed, "rows", split_axis=1, concat_axis=0, tiled=True)
    preact = lax.psum_scatter(
        jnp.dot(shuffled, weight_in, preferred_element_type=F32), "rows", scatter_dimension=0, tiled=True
    )
    hidden = jax.nn.gelu(preact + hidden_bias[None, :], approximate=False).astype(BF16)
    hidden = lax.all_gather(hidden, "rows", axis=0, tiled=True)
    terms = jnp.dot(hidden, weight_out, preferred_element_type=F32)
    terms = lax.all_to_all(terms, "rows", split_axis=0, concat_axis=1, tiled=True)
    branch = lax.psum_scatter(terms, "mp", scatter_dimension=1, tiled=True)
    return (as_float + branch).astype(BF16)


def solution(mesh):
    R, M = mesh.shape["rows"], mesh.shape["mp"]

    def body(tokens, norm_gain, hidden_bias, weight_in, weight_out):
        D = norm_gain.shape[0]
        aligned = tokens.shape[1] % 128 == 0 and weight_in.shape[1] % 512 == 0 and tokens.shape[0] == 16 * sum(sum(group) for group in UNITS)
        if R == 4 and M == 2 * R and aligned and tokens.shape[0] % 128 == 0:
            return fused(tokens, norm_gain, hidden_bias, weight_in, weight_out, R, M, D)
        return plain(tokens, norm_gain, hidden_bias, weight_in, weight_out, R, M, D)

    return jax.shard_map(
        body,
        mesh=mesh,
        in_specs=(P("rows", "mp"), P(), P("mp"), P("rows", "mp"), P("mp", "rows")),
        out_specs=P("rows", "mp"),
        check_vma=False,
    )
```

time: 88.9 us -> 84.5 us (0.951)
  Pallas kernels: 86 us -> 83.4 us
  local copies, waits for them, and re-layouts: 1.62 us -> 0.68 us
    pallas_call x1, Pallas kernels: 86 us -> 83.4 us  [fused(): pl.pallas_call(functools.partial(kernel, R, M, D, groups, schedule(), FAR...]
    unnamed x1, local copies, waits for them, and re-layouts: 1.62 us -> 0.68 us
where the time goes in v3:
time: 84.5 us; the launch traced here: 84.1 us
  Pallas kernels  83.4 us (99%)
    pallas_call x1, Pallas kernels, fused(): pl.pallas_call(functools.partial(kernel, R, M, D, groups, schedule(), FAR...  83.4 us

profile of v3, /device:TPU:0, one launch (start us, length us, event | category | flops | bytes accessed | tf_op | source)
XLA Modules:
  0.0 84.1 jit_solution(10931559314640538703)
XLA Ops:
  0.0 83.4 %shard_map.55 = bf16[128,768]{1,0:T(8,128)(2,1)S(1)} custom-call(bf16[128,768]{1,0:T(8,128)(2,1)} %tok_hbm.1, f32[8,1,768]{2,1,0:T(1,128)} %bitcast.2, f32[1,3072]{1,0:T(1,128)} %bitcast.3, bf16[1536,3072]{1,0:T(8,128)(2,1)} %win_hbm.1, bf16[3072,1536]{1,0:T(8,128)(2,1)} %wout_hbm.1), custom_call_target="tpu_custom_call" | custom-call | tf_op jit(solution)/shard_map/pallas_call | solution.py:506
  83.4 0.7 copy.7

commit v4 on v3

--- a/solution.py
+++ b/solution.py
@@ -11,6 +11,7 @@
 F32 = jnp.float32
 BF16 = jnp.bfloat16
 floor_value = 0.1
+SPLIT = 2
 UNITS = ((1,), (2,), (2,), (1,), (1,), (1,))
 FAR_IN = (2, 3, 4, 5)
 FAR_OUT = (0, 1, 2, 3)
@@ -114,7 +115,13 @@
     def c_r1(k, h, i):
         tile = (first[h], rd)[i]
         return remote(
-            pbuf.at[h, tile, part(k)], r1.at[h, i, part(k)], s_b.at[0], (r_q, r_p)[i].at[k, h], first[h], m
+            pbuf.at[h, :, tile, part(k)], r1.at[h, i, :, part(k)], s_b.at[0], (r_q, r_p)[i].at[k, h], first[h], m
+        )
+
+    def c_r1_half(k, h, i, j):
+        tile = (first[h], rd)[i]
+        return remote(
+            pbuf.at[h, j, tile, part(k)], r1.at[h, i, j, part(k)], s_b.at[0], (r_q, r_p)[i].at[k, h], first[h], m
         )
 
     def c_r2(k, h):
@@ -270,13 +277,25 @@
             in_bias.wait()
 
         tile = half // 2
+
+        def columns(h, j):
+            wat = pl.multiple_of(h * half + j * tile, 128)
+            acc = jnp.dot(nx[0, 0:R * n], win[0:width, pl.ds(wat, tile)], preferred_element_type=F32)
+            acc += jnp.dot(nx[1, 0:R * n], win[width:2 * width, pl.ds(wat, tile)], preferred_element_type=F32)
+            pbuf[h, j, :, span(k)] = acc.astype(BF16).reshape(R, n, tile)
+
+        if k < SPLIT:
+            for j in range(2):
+                for h in range(2):
+                    columns(h, j)
+                    for sub in subs[k]:
+                        c_r1_half(sub, h, 1, j).start()
+                        c_r1_half(sub, h, 0, j).start()
+            return
+
         for h in range(2):
             def col(j, _):
-                at = pl.multiple_of(j * tile, 128)
-                wat = pl.multiple_of(h * half + j * tile, 128)
-                acc = jnp.dot(nx[0, 0:R * n], win[0:width, pl.ds(wat, tile)], preferred_element_type=F32)
-                acc += jnp.dot(nx[1, 0:R * n], win[width:2 * width, pl.ds(wat, tile)], preferred_element_type=F32)
-                pbuf[h, :, span(k), pl.ds(at, tile)] = acc.astype(BF16).reshape(R, n, tile)
+                columns(h, j)
                 return 0
 
             lax.fori_loop(0, 2, col, 0)
@@ -286,17 +305,23 @@
 
     def stage_b1(k):
         for h in range(2):
-            got(r1.at[h, 1, part(k)], r_p.at[k, h])
-            mine = pbuf[h, second[h], part(k)].astype(F32)
-            qbuf[h, part(k)] = (mine + r1[h, 1, part(k)].astype(F32)).astype(BF16)
+            got(r1.at[h, 1, :, part(k)], r_p.at[k, h])
+            for j in range(2):
+                mine = pbuf[h, j, second[h], part(k)].astype(F32)
+                cols = slice(j * (half // 2), (j + 1) * (half // 2))
+                qbuf[h, part(k), cols] = (mine + r1[h, 1, j, part(k)].astype(F32)).astype(BF16)
             c_r2(k, h).start()
 
     def stage_b2(k):
         for h in range(2):
-            got(r1.at[h, :, part(k)], r_q.at[k, h])
-            pre = pbuf[h, r, part(k)].astype(F32) + r1[h, 0, part(k)].astype(F32) + r2[h, part(k)].astype(F32)
-            pre = pre + bias[0:1, h * half:(h + 1) * half]
-            hid[h, r, part(k)] = gelu(pre).astype(BF16)
+            got(r1.at[h, :, :, part(k)], r_q.at[k, h])
+            for j in range(2):
+                cols = slice(j * (half // 2), (j + 1) * (half // 2))
+                pre = pbuf[h, j, r, part(k)].astype(F32) + r1[h, 0, j, part(k)].astype(F32)
+                pre = pre + r2[h, part(k), cols].astype(F32)
+                at = h * half + j * (half // 2)
+                pre = pre + bias[0:1, at:at + half // 2]
+                hid[h, r, part(k), cols] = gelu(pre).astype(BF16)
             c_ag(k, h, 0).start()
             c_ag(k, h, 1).start()
 
@@ -310,7 +335,7 @@
         for sub in subs[k]:
             got(hid.at[:, 0:2, part(sub)], r_ag.at[sub])
 
-        if k == 0:
+        if ("b4", k) == next(stage for stage in order if stage[0] == "b4"):
             pltpu.make_async_copy(wout_hbm, wout, wsem.at[1]).wait()
 
         def product(cc):
@@ -465,25 +490,25 @@
     "send_5 st1_0 a_0",
     "st2_0 m1_0 a_1",
     "m1_1 b1_0 a1_2",
-    "a1_5 b1_1 b2_0",
-    "b2_1 a1_4 a_2",
-    "a1_3 m1_2 b3_0",
-    "b1_2 a_3 b3_1",
-    "m1_3 b2_2 a_4",
-    "b4_0 b1_3 m1_4",
-    "b4_1 c1_1 c1_0",
-    "b3_2 a_5 b2_3",
-    "m1_5 b1_4 b4_2",
-    "b3_3 c1_2 b1_5",
-    "b2_4 b2_5 b4_3",
-    "b3_4 c2_1 c1_3",
-    "c2_0 c2_2 b3_5",
-    "b4_4 c1_4 c2_3",
-    "c4_0 c4_1 b4_5",
-    "c4_2 c1_5 c2_4",
-    "c4_3 c2_5 c3_0",
-    "c3_3 c3_2 c3_4",
-    "c3_1 c3_5 e_0",
+    "b1_1 a1_5 a1_3",
+    "a1_4 b2_0 b2_1",
+    "a_2 m1_2 b3_0",
+    "b1_2 b3_1 a_5",
+    "a_3 m1_3 b2_2",
+    "a_4 m1_4 b4_1",
+    "c1_1 b1_3 b3_2",
+    "m1_5 b1_4 b2_3",
+    "b4_0 b4_2 c1_0",
+    "b1_5 c1_2 b2_4",
+    "b3_3 b2_5 b3_4",
+    "c2_0 c2_1 b4_3",
+    "c1_3 b3_5 c2_2",
+    "b4_4 c4_0 c1_4",
+    "b4_5 c4_1 c2_3",
+    "c1_5 c4_2 c2_4",
+    "c3_0 c4_3 c2_5",
+    "c3_4 c3_1 c3_2",
+    "c3_3 c3_5 e_0",
 )
 
 
@@ -512,7 +537,7 @@
             V(tokens.shape, BF16), V((M, 1, width), F32), V((1, ff), F32), V(weight_in.shape, BF16), V(weight_out.shape, BF16),
             V((2, R, height, width), BF16), V((2, R * max(sum(group) for group in groups), width), BF16),
             V((M, 8, height), F32), V((R, 8, height), F32), V((R, height, 128), F32),
-            V((2, R, height, half), BF16), V((2, 2, height, half), BF16), V((2, height, half), BF16),
+            V((2, 2, R, height, half // 2), BF16), V((2, 2, 2, height, half // 2), BF16), V((2, height, half), BF16),
             V((2, height, half), BF16), V((2, R, height, half), BF16),
             V((R, height, width), BF16), V((R, height, width), BF16), V((R, height, width), F32),
             V((R, height, width), BF16), V((R, height, width), BF16), V((R, height, width), BF16),

time: 84.5 us -> 84.1 us (level)
  no operation moved by 1% of the time
where the time goes in v4:
time: 84.1 us; the launch traced here: 83.3 us
  Pallas kernels  82.6 us (98%)
    pallas_call x1, Pallas kernels, fused(): pl.pallas_call(functools.partial(kernel, R, M, D, groups, schedule(), FAR...  82.6 us

profile of v4, /device:TPU:0, one launch (start us, length us, event | category | flops | bytes accessed | tf_op | source)
XLA Modules:
  0.0 83.3 jit_solution(4881439575754429564)
XLA Ops:
  0.0 82.6 %shard_map.55 = bf16[128,768]{1,0:T(8,128)(2,1)S(1)} custom-call(bf16[128,768]{1,0:T(8,128)(2,1)} %tok_hbm.1, f32[8,1,768]{2,1,0:T(1,128)} %bitcast.2, f32[1,3072]{1,0:T(1,128)} %bitcast.3, bf16[1536,3072]{1,0:T(8,128)(2,1)} %win_hbm.1, bf16[3072,1536]{1,0:T(8,128)(2,1)} %wout_hbm.1), custom_call_target="tpu_custom_call" | custom-call | tf_op jit(solution)/shard_map/pallas_call | solution.py:531
  82.6 0.7 copy.7
